TPU v7x, 128 devices: a whole 4x4x4 slice. The times are simulated.
128 devices in a mesh: seq: 16 (over y, x), head: 8 (over z, core).
Axes of the slice: x: 4, y: 4, z: 4, core: 2. Of those that a mesh axis runs over, the one named last changes fastest.
Arguments:
- queries: bfloat16 [4096, 16384], P('seq', 'head'), may hold values from -6 to 6
- keys: bfloat16 [4096, 1024], P('seq', 'head'), may hold values from -6 to 6
- values: bfloat16 [4096, 1024], P('seq', 'head'), may hold values from -6 to 6
- teacher: bfloat16 [4096, 16384], P('seq', 'head'), may hold values from -17 to 17
- map_q: bfloat16 [128, 128, 64], P('head'), may hold values from -0.5 to 0.5
- map_k: bfloat16 [128, 128, 64], P('head'), may hold values from -0.5 to 0.5
Outputs:
- grad_map_q: float32 [128, 128, 64], P('head', 'seq')
- grad_map_k: float32 [128, 128, 64], P('head', 'seq')
All inputs are finite; a program needn't handle non-finite values.
Results may differ from a plain program's by a relative error of at most 0.0003.
Values sent between devices are 32-bit elements; how exact they have to be, the bound alone decides.
A program may use at most 128 MiB of HBM per device.

v0:
```python
import jax
import jax.numpy as jnp
from jax import lax
from jax.sharding import Mesh
from jax.sharding import PartitionSpec as P

HEADS = 128
DH = 128
BLOCK = 256
SEQ = ("seq_0", "seq_1")


exact_mode = lax.Precision.HIGHEST


def neutral_like(array, identity):
    return jax.tree.map(
        lambda part, zero: jnp.zeros_like(part) + jnp.asarray(zero, part.dtype), array, identity
    )


def prefix_by_axis(array, axes, combine, identity, reverse):
    before = start = neutral_like(array, identity)
    total = array
    for axis in reversed(axes):
        length, index = (lax.axis_size(axis), lax.axis_index(axis))
        pieces = jax.tree.map(lambda part: lax.all_gather(part, axis), total)
        inside, total = (start, start)
        for k in reversed(range(length)) if reverse else range(length):
            passed = k > index if reverse else k < index
            total = combine(total, jax.tree.map(lambda part: part[k], pieces))
            inside = jax.tree.map(lambda new, old: jnp.where(passed, new, old), total, inside)
        before = combine(inside, before)
    return before


def split_up(array, dim, length):
    shape = array.shape
    pieces = array.reshape(*shape[:dim], length, shape[dim] // length, *shape[dim + 1 :])
    return jnp.moveaxis(pieces, dim, 0)


def summed_on_arrival(array, axis, dim):
    pieces = split_up(array, dim, lax.axis_size(axis))
    arrived = lax.all_to_all(pieces, axis, split_axis=0, concat_axis=0, tiled=True)
    return arrived.sum(axis=0)


def halves(inputs, weight):
    logits = jnp.einsum("nhld,hdf->nhlf", inputs, weight, preferred_element_type=jnp.float32)
    positive = jnp.exp(logits)
    negative = jnp.exp(-logits)
    up_soft = positive / jnp.sum(positive, -1, keepdims=True)
    down_soft = negative / jnp.sum(negative, -1, keepdims=True)
    return (up_soft, down_soft)


def map_grad(inputs, up_soft, down_soft, grad_feat, half_width):
    grad_up = grad_feat[..., :half_width]
    grad_down = grad_feat[..., half_width:]
    grad_logit = up_soft * (grad_up - jnp.sum(up_soft * grad_up, -1, keepdims=True))
    grad_logit = grad_logit - down_soft * (
        grad_down - jnp.sum(down_soft * grad_down, -1, keepdims=True)
    )
    return jnp.einsum(
        "nhld,nhlf->hdf", inputs.astype(jnp.float32), grad_logit, precision=exact_mode
    )


def add_pair(earlier, later):
    return (earlier[0] + later[0], earlier[1] + later[1])


def on_device(queries, keys, values, teacher, map_q, map_k):
    head_count = map_q.shape[0]
    head_width = map_q.shape[1]
    half_width = map_q.shape[2]
    tokens = queries.shape[0]
    block_count = tokens // BLOCK
    shared_count = keys.shape[1] // head_width
    group_size = head_count // shared_count

    def blocked(source, count):
        return source.reshape(block_count, BLOCK, count, head_width).transpose(0, 2, 1, 3)

    query_blk = blocked(queries, head_count)
    key_blk = jnp.repeat(blocked(keys, shared_count), group_size, axis=1)
    value_blk = jnp.repeat(blocked(values, shared_count), group_size, axis=1)
    teacher_blk = blocked(teacher, head_count)
    local_power = jnp.sum(jnp.square(teacher.astype(jnp.float32)), axis=1)
    power = lax.psum(local_power, "head") / (HEADS * DH) + 1e-05
    power_blk = power.reshape(block_count, BLOCK)
    q_up, q_down = halves(query_blk, map_q)
    k_up, k_down = halves(key_blk, map_k)
    query_feat = jnp.concatenate([q_up, q_down], -1)
    key_feat = jnp.concatenate([k_up, k_down], -1)
    local_state = jnp.einsum(
        "nhlf,nhld->hfd", key_feat, value_blk.astype(jnp.float32), precision=exact_mode
    )
    local_total = jnp.sum(key_feat, axis=(0, 2))
    zero_state = jnp.zeros_like(local_state)
    zero_total = jnp.zeros_like(local_total)
    state_start, total_start = prefix_by_axis(
        (local_state, local_total), SEQ, add_pair, (zero_state, zero_total), False
    )
    causal = jnp.tril(jnp.ones((BLOCK, BLOCK), jnp.float32))

    def forward(carried, blocks):
        kv_state, key_total = carried
        q_cur, k_cur, v_cur, t_cur, p_cur = blocks
        v_float = v_cur.astype(jnp.float32)
        scores = jnp.einsum("hqf,hkf->hqk", q_cur, k_cur, precision=exact_mode) * causal
        numerator = jnp.einsum("hqf,hfd->hqd", q_cur, kv_state, precision=exact_mode)
        numerator = numerator + jnp.einsum("hqk,hkd->hqd", scores, v_float, precision=exact_mode)
        denominator = jnp.einsum("hqf,hf->hq", q_cur, key_total, precision=exact_mode) + jnp.sum(
            scores, -1
        )
        student = numerator / denominator[..., None]
        grad_out = (student - t_cur.astype(jnp.float32)) / p_cur[None, :, None]
        grad_numer = grad_out / denominator[..., None]
        grad_denom = -jnp.sum(grad_out * student, -1) / denominator
        back_scores = (
            jnp.einsum("hqd,hkd->hqk", grad_numer, v_float, precision=exact_mode)
            + grad_denom[..., None]
        ) * causal
        grad_qfeat = jnp.einsum("hfd,hqd->hqf", kv_state, grad_numer, precision=exact_mode)
        grad_qfeat = grad_qfeat + grad_denom[..., None] * key_total[:, None, :]
        grad_qfeat = grad_qfeat + jnp.einsum(
            "hqk,hkf->hqf", back_scores, k_cur, precision=exact_mode
        )
        new_state = kv_state + jnp.einsum("hkf,hkd->hfd", k_cur, v_float, precision=exact_mode)
        return ((new_state, key_total + jnp.sum(k_cur, 1)), (grad_qfeat, grad_numer, grad_denom))

    _, (grad_qfeat, grad_numer, grad_denom) = lax.scan(
        forward,
        (state_start, total_start),
        (query_feat, key_feat, value_blk, teacher_blk, power_blk),
    )
    local_gstate = jnp.einsum("nhlf,nhld->hfd", query_feat, grad_numer, precision=exact_mode)
    local_gtotal = jnp.einsum("nhlf,nhl->hf", query_feat, grad_denom, precision=exact_mode)
    gstate_end, gtotal_end = prefix_by_axis(
        (local_gstate, local_gtotal), SEQ, add_pair, (zero_state, zero_total), True
    )

    def backward(carried, blocks):
        grad_state, grad_total = carried
        q_cur, k_cur, v_cur, gn_cur, gd_cur = blocks
        v_float = v_cur.astype(jnp.float32)
        back_scores = (
            jnp.einsum("hqd,hkd->hqk", gn_cur, v_float, precision=exact_mode) + gd_cur[..., None]
        ) * causal
        grad_kfeat = jnp.einsum("hqk,hqf->hkf", back_scores, q_cur, precision=exact_mode)
        grad_kfeat = grad_kfeat + jnp.einsum(
            "hfd,hkd->hkf", grad_state, v_float, precision=exact_mode
        )
        grad_kfeat = grad_kfeat + grad_total[:, None, :]
        new_grad = grad_state + jnp.einsum("hqf,hqd->hfd", q_cur, gn_cur, precision=exact_mode)
        new_total = grad_total + jnp.einsum("hqf,hq->hf", q_cur, gd_cur, precision=exact_mode)
        return ((new_grad, new_total), grad_kfeat)

    _, grad_kfeat = lax.scan(
        backward,
        (gstate_end, gtotal_end),
        (query_feat, key_feat, value_blk, grad_numer, grad_denom),
        reverse=True,
    )
    local_gq = map_grad(query_blk, q_up, q_down, grad_qfeat, half_width)
    local_gk = map_grad(key_blk, k_up, k_down, grad_kfeat, half_width)
    grad_map_q, grad_map_k = (
        summed_on_arrival(local_gq, SEQ, 1),
        summed_on_arrival(local_gk, SEQ, 1),
    )
    return (grad_map_q, grad_map_k)


def solution(mesh):
    finer = Mesh(mesh.devices.reshape(4, 4, mesh.shape["head"]), ("seq_0", "seq_1", "head"))
    placed = (
        P(SEQ, "head"),
        P(SEQ, "head"),
        P(SEQ, "head"),
        P(SEQ, "head"),
        P("head", None, None),
        P("head", None, None),
    )
    return jax.shard_map(
        on_device,
        mesh=finer,
        in_specs=placed,
        out_specs=(P("head", SEQ, None), P("head", SEQ, None)),
        check_vma=False,
    )
```

profile of v0, /device:TPU:0, one launch (start us, length us, event | category | flops | bytes accessed | tf_op | source)
XLA Modules:
  0.0 277.2 jit_solution(782148218267800317)
XLA Ops:
  12.0 50.8 %all-gather.13.cloned.1.call-done = f32[64,128,128]{2,1,0:T(8,128)} async-done(((f32[16,128,128]{2,1,0:T(8,128)}), f32[64,128,128]{2,1,0:T(8,128)}) %all-gather.13.cloned.1.call-update) | async-done | bytes 4194320 | tf_op jit(solution)/shard_map/all_gather | solution.py:27
  62.8 3.4 %fusion.26 = f32[1,16,128,128]{3,2,1,0:T(8,128)} fusion(f32[64,128,128]{2,1,0:T(8,128)} %all-gather.13.cloned.1.call-done), kind=kLoop, calls=%fused_computation.45 | loop fusion | flops 786432 | bytes 5242880 | tf_op jit(solution)/shard_map/add | solution.py:71
  66.3 2.6 copy.72
  70.9 15.2 %psum.7 = f32[256]{0:T(256)S(1)} all-reduce(f32[256]{0:T(256)S(1)} %multiply_reduce_fusion.2), channel_id=1, replica_groups=mesh['seq_0'=4,'seq_1'=4,'head'=8] {'head'}, use_global_device_ids=true, to_apply=%region_7.8 | all-reduce | flops 256 | bytes 2048 | tf_op jit(solution)/shard_map/psum | solution.py:91
  86.4 11.9 %all-gather.1 = f32[64,128]{1,0:T(8,128)S(1)} all-gather(f32[16,128]{1,0:T(8,128)S(1)} %fusion.54), channel_id=3, replica_groups=mesh['seq_0'=4,'seq_1'=4,'head'=8] {'seq_1'}, dimensions={0}, use_global_device_ids=true | all-gather | bytes 40960 | tf_op jit(solution)/shard_map/all_gather | solution.py:27
  98.3 12.5 %all_gather.45 = f32[4,16,128]{2,1,0:T(8,128)S(1)} all-gather(f32[1,16,128]{2,1,0:T(8,128)S(1)} %fusion.90), channel_id=1, replica_groups=mesh['seq_0'=4,'seq_1'=4,'head'=8] {'seq_0'}, dimensions={0}, use_global_device_ids=true | all-gather | bytes 40960 | tf_op jit(solution)/shard_map/all_gather | solution.py:27
  113.1 3.7 %multiply_reduce_fusion = (f32[16,256]{1,0:T(8,128)S(1)}, f32[16,256,256]{1,2,0:T(8,128)S(1)}) fusion(f32[256,256]{0,1:T(8,128)S(1)} %fusion.79, f32[1,16,256,64]{2,3,1,0:T(8,128)S(1)} %copy-done.2, f32[1,16,256,64]{2,3,1,0:T(8,128)S(1)} %get-tuple-element.66, f32[1,16,256,64]{2,3,1,0:T(8,128)S(1)} %get-tuple-element.69, ...), kind=kOutput, calls=%fused_computation.1 | convolution fusion | flops 1613754368 | bytes 8667136 | tf_op jit(solution)/shard_map/while/body/eval_jaxpr/hqf,hkf->hqk/dot_general | solution.py:112
  116.8 3.3 %fusion = f32[16,256,128]{1,2,0:T(8,128)} fusion(f32[16,256,256]{1,2,0:T(8,128)S(1)} %get-tuple-element.73, f32[256,256]{0,1:T(8,128)S(1)} %fusion.79, bf16[256,128]{1,0:T(8,128)(2,1)S(1)} %copy-done.17), kind=kOutput, calls=%fused_computation.2 | convolution fusion | flops 1611661312 | bytes 6619136 | tf_op jit(solution)/shard_map/while/body/eval_jaxpr/hqk,hkd->hqd/dot_general | solution.py:114
  120.1 4.5 %fusion.25 = f32[16,128,128]{2,1,0:T(8,128)S(1)} fusion(f32[4,16,128,128]{3,2,1,0:T(8,128)} %all-gather.9.cloned.1.call-done, f32[64,128,128]{2,1,0:T(8,128)} %all-gather.13.cloned.1.call-done, pred[]{:T(512)S(6)} %gt.29, pred[]{:T(512)S(6)} %gt.30, pred[]{:T(512)S(6)} %gt.31, pred[]{:T(512)S(6)} %gt.28, pred[]{:T(512)S(6)} %gt.27, pred[]{:T(512)S(6)} %gt.26, ...), kind=kLoop, calls=%fused_computation.41 | loop fusion | flops 3932160 | bytes 9437192 | tf_op jit(solution)/shard_map/add | solution.py:71
  124.7 2.8 %multiply_reduce_fusion.1 = (f32[16,256]{1,0:T(8,128)S(1)}, f32[16,256,128]{1,2,0:T(8,128)S(1)}) fusion(f32[256]{0:T(256)S(1)} %multiply_add_fusion, f32[256,2048]{0,1:T(8,128)S(1)} %copy-done.16, f32[16,256]{1,0:T(8,128)S(1)} %bitcast_add_fusion.1, f32[16,256,128]{1,2,0:T(8,128)S(1)} %bitcast.146, f32[16,256,128]{1,2,0:T(8,128)S(1)} %copy-done.15, ...), kind=kOutput, calls=%fused_computation.19 | convolution fusion | flops 810545152 | bytes 11568128 | tf_op jit(solution)/shard_map/while/body/eval_jaxpr/hqf,hfd->hqd/dot_general | solution.py:113
  129.0 3.5 %fusion.81 = f32[16,128,128]{2,1,0:T(8,128)} fusion(f32[16,256,128]{1,2,0:T(8,128)S(1)} %get-tuple-element.56, f32[1,16,256,64]{2,3,1,0:T(8,128)S(1)} %get-tuple-element.69, f32[1,16,256,64]{2,3,1,0:T(8,128)S(1)} %get-tuple-element.68), kind=kOutput, calls=%fused_computation.119 | convolution fusion | flops 805830656 | bytes 5242880 | tf_op jit(solution)/shard_map/nhlf,nhld->hfd/dot_general | solution.py:139
  132.5 45.2 %all-gather.15.cloned.1.call-done = f32[64,128,128]{2,1,0:T(8,128)} async-done(((f32[16,128,128]{2,1,0:T(8,128)}), f32[64,128,128]{2,1,0:T(8,128)}) %all-gather.15.cloned.1.call-update) | async-done | bytes 4194320 | tf_op jit(solution)/shard_map/all_gather | solution.py:27
  177.7 3.5 %fusion.22 = f32[1,16,128,128]{3,2,1,0:T(8,128)} fusion(f32[64,128,128]{2,1,0:T(8,128)} %all-gather.15.cloned.1.call-done), kind=kLoop, calls=%fused_computation.35 | loop fusion | flops 786432 | bytes 5242880 | tf_op jit(solution)/shard_map/add | solution.py:71
  181.2 4.0 %fusion.100 = f32[16,256,128]{1,2,0:T(8,128)S(1)} fusion(f32[16,256,128]{1,2,0:T(8,128)} %copy-done.6, f32[16,128,128]{2,1,0:T(8,128)} %copy-done.11), kind=kOutput, calls=%fused_computation.155 | convolution fusion | flops 805306368 | bytes 5242880 | tf_op jit(solution)/shard_map/while/body/eval_jaxpr/hfd,hqd->hqf/dot_general | solution.py:126
  187.2 3.4 %add_bitcast_fusion = f32[1,16,256,128]{2,3,1,0:T(8,128)S(1)} fusion(f32[16,256,128]{1,2,0:T(8,128)S(1)} %fusion.100, f32[16,256,256]{1,2,0:T(8,128)S(1)} %fusion.64, f32[16,256]{1,0:T(8,128)S(1)} %negate_divide_fusion, f32[256,256]{0,1:T(8,128)S(1)} %copy-done.9, f32[16,128]{1,0:T(8,128)S(1)} %bitcast.150, f32[1,16,256,64]{2,3,1,0:T(8,128)S(1)} %copy-done.3, ...), kind=kOutput, calls=%fused_computation.16 | convolution fusion | flops 1614807040 | bytes 10772480 | tf_op jit(solution)/shard_map/while/body/eval_jaxpr/hqk,hkf->hqf/dot_general | solution.py:128
  198.5 2.7 reshape.408
  201.2 6.0 %all-to-all-start = ((f32[16,1,8192]{2,1,0:T(1,128)}), f32[16,1,8192]{2,1,0:T(1,128)}, u32[]{:S(2)}, u32[]{:S(2)}) async-start(f32[16,1,8192]{2,1,0:T(1,128)} %reshape.408), calls=%async_computation | async-start | bytes 1048576 | tf_op jit(solution)/shard_map/all_to_all | solution.py:45
  209.0 13.2 %all-gather.3 = f32[64,128]{1,0:T(8,128)S(1)} all-gather(f32[16,128]{1,0:T(8,128)S(1)} %bitcast.151), channel_id=5, replica_groups=mesh['seq_0'=4,'seq_1'=4,'head'=8] {'seq_1'}, dimensions={0}, use_global_device_ids=true | all-gather | bytes 40960 | tf_op jit(solution)/shard_map/all_gather | solution.py:27
  222.2 12.8 %all_gather.51 = f32[4,16,128]{2,1,0:T(8,128)S(1)} all-gather(f32[1,16,128]{2,1,0:T(8,128)S(1)} %fusion.87), channel_id=1, replica_groups=mesh['seq_0'=4,'seq_1'=4,'head'=8] {'seq_0'}, dimensions={0}, use_global_device_ids=true | all-gather | bytes 40960 | tf_op jit(solution)/shard_map/all_gather | solution.py:27
  235.0 8.3 %fusion.2 = f32[16,256,128]{1,2,0:T(8,128)} fusion(f32[16,256,256]{1,2,0:T(8,128)} %copy-done.5, f32[16,256]{1,0:T(8,128)S(1)} %negate_divide_fusion, f32[256,256]{0,1:T(8,128)S(1)} %copy-done.10, f32[1,16,256,64]{2,3,1,0:T(8,128)S(1)} %get-tuple-element.69, f32[1,16,256,64]{2,3,1,0:T(8,128)S(1)} %get-tuple-element.68), kind=kOutput, calls=%fused_computation.4 | convolution fusion | flops 1613234176 | bytes 8667136 | tf_op jit(solution)/shard_map/while/body/eval_jaxpr/hqk,hqf->hkf/dot_general | solution.py:152
  243.4 5.4 %fusion.5 = f32[1,16,256,128]{2,3,1,0:T(8,128)S(1)} fusion(f32[16,256,128]{1,2,0:T(8,128)} %fusion.2, f32[4,16,128,128]{3,2,1,0:T(8,128)} %all-gather.11.cloned.1.call-done, f32[1,16,128,128]{3,2,1,0:T(8,128)} %fusion.22, f32[16,128]{1,0:T(8,128)S(1)} %fusion.86, f32[64,128,128]{2,1,0:T(8,128)} %all-gather.15.cloned.1.call-done, ...), kind=kOutput, calls=%fused_computation.10 | convolution fusion | flops 810024960 | bytes 12656648 | tf_op jit(solution)/shard_map/while/body/eval_jaxpr/hfd,hkd->hkf/dot_general | solution.py:153
  252.3 4.9 %all-to-all-start.1 = ((f32[16,1,8192]{2,1,0:T(1,128)}), f32[16,1,8192]{2,1,0:T(1,128)S(1)}, u32[]{:S(2)}, u32[]{:S(2)}) async-start(f32[16,1,8192]{2,1,0:T(1,128)} %reshape.410), calls=%async_computation.1 | async-start | bytes 1048576 | tf_op jit(solution)/shard_map/all_to_all | solution.py:45
  257.8 2.9 %reduce.8 = f32[16,8192]{1,0:T(8,128)S(1)} reduce(f32[16,1,8192]{2,1,0:T(1,128)} %all-to-all-done, f32[]{:T(128)} %broadcast.251), dimensions={1}, to_apply=%all_to_all.6.reduce_sub_computation | reduce | bytes 1048580 | tf_op jit(solution)/shard_map/all_to_all | solution.py:45
  261.9 5.5 %all-to-all-done.1 = f32[16,1,8192]{2,1,0:T(1,128)S(1)} async-done(((f32[16,1,8192]{2,1,0:T(1,128)}), f32[16,1,8192]{2,1,0:T(1,128)S(1)}, u32[]{:S(2)}, u32[]{:S(2)}) %all-to-all-start.1) | async-done | bytes 524320 | tf_op jit(solution)/shard_map/all_to_all | solution.py:45
  (85 shorter events, 30.8 us)
Async XLA Ops:
  7.2 2.7 copy-start.17
  7.2 55.6 %all-gather.13.cloned.1.call-start = ((), (), s32[]{:S(2)}) async-start(), calls=%async_computation.4 | async-start | bytes 5242880 | tf_op jit(solution)/shard_map/all_gather | solution.py:27
  9.9 76.2 %copy-start.1 = (f32[1,16,256,64]{2,3,1,0:T(8,128)}, f32[1,16,256,64]{2,3,1,0:T(8,128)S(1)}, u32[]{:S(2)}) copy-start(f32[1,16,256,64]{2,3,1,0:T(8,128)S(1)} %get-tuple-element.67) | copy-start | bytes 3145732
  12.0 108.1 %all-gather.9.cloned.1.call-start = ((), (), s32[]{:S(2)}) async-start(), calls=%async_computation.2 | async-start | bytes 5242880 | tf_op jit(solution)/shard_map/all_gather | solution.py:27
  66.2 2.7 copy-start.12
  66.3 111.4 %all-gather.15.cloned.1.call-start = ((), (), s32[]{:S(2)}) async-start(), calls=%async_computation.5 | async-start | bytes 5242880 | tf_op jit(solution)/shard_map/all_gather | solution.py:27
  70.9 40.0 %copy-start.13 = (bf16[32,8,16,128]{3,2,1,0:T(8,128)(2,1)S(1)}, bf16[32,8,16,128]{3,2,1,0:T(8,128)(2,1)}, u32[]{:S(2)}) copy-start(bf16[32,8,16,128]{3,2,1,0:T(8,128)(2,1)} %copy.72) | copy-start | bytes 3145732
  86.1 24.9 %copy-start.19 = (bf16[16,128,64]{1,2,0:T(8,128)(2,1)S(1)}, bf16[16,128,64]{1,2,0:T(8,128)(2,1)}, u32[]{:S(2)}) copy-start(bf16[16,128,64]{1,2,0:T(8,128)(2,1)} %param.10) | copy-start | bytes 786436
  110.9 5.9 %copy-start.8 = (f32[256,256]{0,1:T(8,128)}, f32[256,256]{0,1:T(8,128)S(1)}, u32[]{:S(2)}) copy-start(f32[256,256]{0,1:T(8,128)S(1)} %fusion.79) | copy-start | bytes 786436
  111.5 1.5 copy-start.2
  120.1 4.5 %copy-start.15 = (f32[16,256,128]{1,2,0:T(8,128)S(1)}, f32[16,256,128]{1,2,0:T(8,128)}, u32[]{:S(2)}) copy-start(f32[16,256,128]{1,2,0:T(8,128)} %fusion) | copy-start | bytes 6291460
  120.1 4.7 %copy-start.16 = (f32[256,2048]{0,1:T(8,128)S(1)}, f32[256,2048]{0,1:T(8,128)}, u32[]{:S(2)}) copy-start(f32[256,2048]{0,1:T(8,128)} %copy.45) | copy-start | bytes 6291460
  124.6 3.0 %copy-start.11 = (f32[16,128,128]{2,1,0:T(8,128)}, f32[16,128,128]{2,1,0:T(8,128)S(1)}, u32[]{:S(2)}) copy-start(f32[16,128,128]{2,1,0:T(8,128)S(1)} %fusion.25) | copy-start | bytes 3145732
  127.6 1.4 copy-start.6
  132.5 110.9 %all-gather.11.cloned.1.call-start = ((), (), s32[]{:S(2)}) async-start(), calls=%async_computation.3 | async-start | bytes 5242880 | tf_op jit(solution)/shard_map/all_gather | solution.py:27
  181.2 4.0 %copy-start.7 = (f32[16,256,128]{1,2,0:T(8,128)S(1)}, f32[16,256,128]{1,2,0:T(8,128)}, u32[]{:S(2)}) copy-start(f32[16,256,128]{1,2,0:T(8,128)} %copy-done.6) | copy-start | bytes 6291460
  185.2 1.9 copy-start.3
  185.2 1.9 copy-start.9
  187.2 3.4 %copy-start.5 = (f32[16,256,256]{1,2,0:T(8,128)}, f32[16,256,256]{1,2,0:T(8,128)S(1)}, u32[]{:S(2)}) copy-start(f32[16,256,256]{1,2,0:T(8,128)S(1)} %fusion.64) | copy-start | bytes 12582916
  190.6 1.3 copy-start.14
  201.2 51.2 %all-to-all-start = ((f32[16,1,8192]{2,1,0:T(1,128)}), f32[16,1,8192]{2,1,0:T(1,128)}, u32[]{:S(2)}, u32[]{:S(2)}) async-start(f32[16,1,8192]{2,1,0:T(1,128)} %reshape.408), calls=%async_computation | async-start | bytes 1048576 | tf_op jit(solution)/shard_map/all_to_all | solution.py:45
  207.1 27.9 %copy-start.10 = (f32[256,256]{0,1:T(8,128)S(1)}, f32[256,256]{0,1:T(8,128)}, u32[]{:S(2)}) copy-start(f32[256,256]{0,1:T(8,128)} %copy-done.8) | copy-start | bytes 786436
  243.4 5.4 %copy-start.4 = (f32[1,16,256,64]{2,3,1,0:T(8,128)S(1)}, f32[1,16,256,64]{2,3,1,0:T(8,128)}, u32[]{:S(2)}) copy-start(f32[1,16,256,64]{2,3,1,0:T(8,128)} %copy-done.1) | copy-start | bytes 3145732
  252.3 15.1 %all-to-all-start.1 = ((f32[16,1,8192]{2,1,0:T(1,128)}), f32[16,1,8192]{2,1,0:T(1,128)S(1)}, u32[]{:S(2)}, u32[]{:S(2)}) async-start(f32[16,1,8192]{2,1,0:T(1,128)} %reshape.410), calls=%async_computation.1 | async-start | bytes 1048576 | tf_op jit(solution)/shard_map/all_to_all | solution.py:45
  (2 other events, 1.8 us)
Sparse Core Ops, SparseCore 0:
  12.1 50.6 all-gather.12
  66.4 48.8 all-gather.8
  132.6 45.0 all-gather.14
  181.3 54.4 all-gather.10
where the time goes:
time: 281 us; the launch traced here: 277 us
  waiting for transfers between devices  102 us (36%)
  blocking collectives  65.6 us (23%)
  matrix products  46 us (16%)
  other arithmetic  20.1 us (7%)
  local copies, waits for them, and re-layouts  18.5 us (7%)
  between operations  14.4 us (5%)
  starting transfers between devices  11.1 us (4%)
    all_gather x4, waiting for transfers between devices, prefix_by_axis(): pieces = jax.tree.map(lambda part: lax.all_gather(part, axis), total)  95.9 us
    all_gather x4, blocking collectives, prefix_by_axis(): pieces = jax.tree.map(lambda part: lax.all_gather(part, axis), total)  50.4 us
    psum x1, blocking collectives, on_device(): power = lax.psum(local_power, 'head') / (HEADS * DH) + 1e-05  15.2 us
    add x7, other arithmetic, add_pair(): return (earlier[0] + later[0], earlier[1] + later[1])  11.4 us
    unnamed x45, local copies, waits for them, and re-layouts  11.1 us
    all_to_all x2, starting transfers between devices, summed_on_arrival(): lax.all_to_all(pieces, axis, split_axis=0, concat_axis=0, tiled=True)  10.9 us
    dot_general x1, matrix products, backward(): jnp.einsum('hqk,hqf->hkf', back_scores, q_cur, precision=exact_mode)  8.35 us
  transfers between devices with their start and end apart: 6, of which 3 were waited for; matrix products, arithmetic and copies ran while one was open for 20% of the time, Pallas kernels for 0%

commit v1 on v0

v1 whole, which is shorter than its diff:
```python
import functools

import jax
import jax.numpy as jnp
from jax import lax
from jax.experimental import pallas as pl
from jax.experimental.pallas import tpu as pltpu
from jax.sharding import PartitionSpec as P

HEADS = 128
DH = 128
FH = 64
T = 256
NS = 16
NH = 8
ROWS = 136
MESH = pl.DeviceIdType.MESH
F32 = jnp.float32
BF16 = jnp.bfloat16


def split(x):
    high = x.astype(BF16)
    return high, (x - high.astype(F32)).astype(BF16)


def cols(x, y):
    return jnp.concatenate([x, y], axis=1)


def dot(a, b):
    return jnp.dot(a, b, preferred_element_type=F32)


def dot_t(a, b):
    return lax.dot_general(a, b, (((1,), (1,)), ((), ())), preferred_element_type=F32)


def fold(x):
    return x[:, :128] + x[:, 128:]


def kernel(
    q, k, v, t, mq, mk, oq, ok,
    khl, qhl, ghl, ni, dp, gd_s, rp, vta, vv, kt_s, bb,
    p_send, p_recv, a_send, a_recv, c_send, c_recv, d_send, d_recv, f_send, f_recv,
    gq_send, gq_recv, gk_send, gk_recv,
    ss, rs, pss, prs,
):
    me = lax.axis_index("seq")
    hd = lax.axis_index("head")

    barrier = pltpu.get_barrier_semaphore()
    for j in range(1, NS):
        pl.semaphore_signal(
            barrier, inc=1, device_id={"seq": lax.rem(me + j, NS)}, device_id_type=MESH
        )
    for j in range(1, NH):
        pl.semaphore_signal(
            barrier, inc=1, device_id={"head": lax.rem(hd + j, NH)}, device_id_type=MESH
        )

    def seq_copy(phase, src, dst_buf, dst, slot):
        return pltpu.make_async_remote_copy(
            src_ref=src,
            dst_ref=dst_buf.at[slot],
            send_sem=ss.at[phase, dst],
            recv_sem=rs.at[phase, slot],
            device_id={"seq": dst},
            device_id_type=MESH,
        )

    def arrived(phase, buf, slot):
        pltpu.make_async_remote_copy(
            src_ref=buf.at[slot],
            dst_ref=buf.at[slot],
            send_sem=ss.at[phase, slot],
            recv_sem=rs.at[phase, slot],
            device_id={"seq": slot},
            device_id_type=MESH,
        ).wait_recv()

    def power_copy(dst, slot):
        return pltpu.make_async_remote_copy(
            src_ref=p_send,
            dst_ref=p_recv.at[slot],
            send_sem=pss.at[dst],
            recv_sem=prs.at[slot],
            device_id={"head": dst},
            device_id_type=MESH,
        )

    def head_cols(ref, h):
        return ref[:, pl.ds(pl.multiple_of(h * DH, DH), DH)]

    row = lax.broadcasted_iota(jnp.int32, (2 * DH, DH), 0)
    col = lax.broadcasted_iota(jnp.int32, (2 * DH, DH), 1)
    bb[...] = jnp.where(lax.rem(row, DH) // FH == col // FH, 1.0, 0.0).astype(BF16)
    causal = lax.broadcasted_iota(jnp.int32, (T, T), 0) >= lax.broadcasted_iota(
        jnp.int32, (T, T), 1
    )
    vta[:DH] = v[...].T
    vta[DH:] = jnp.ones((16, T), BF16)
    vv[...] = cols(v[...], v[...])
    kt_s[...] = k[...].T

    def seg_sum(x):
        return dot(cols(*split(x)), bb[...])

    def features(x, m):
        e = jnp.exp(dot(x, cols(m, -m)))
        return cols(*split(e * (1.0 / seg_sum(e))))

    def stage_a(j, _):
        h = lax.rem(me + 1 + j, NS)
        f = features(k[...], mk[h])
        khl[h] = f
        a_send[h] = fold(dot(vta[...], f))[:ROWS]

        @pl.when(j == 0)
        def _():
            pl.semaphore_wait(barrier, NS + NH - 2)

        @pl.when(j < NS - 1)
        def _():
            seq_copy(0, a_send.at[h], a_recv, h, me).start()

        return 0

    lax.fori_loop(0, NS, stage_a, 0)
    a_recv[me] = a_send[me]

    def squares(j, total):
        x = head_cols(t, j).astype(F32)
        return total + x * x

    sq = lax.fori_loop(0, NS, squares, jnp.zeros((T, DH), F32))
    p_send[...] = jnp.broadcast_to(jnp.sum(sq.T, axis=0, keepdims=True), (8, T))
    for j in range(1, NH):
        power_copy(lax.rem(hd + j, NH), hd).start()

    def stage_b(h, _):
        f = features(head_cols(q, h), mq[h])
        qhl[h] = f
        g = khl[h]
        gh = g[:, :DH]
        s = dot_t(f, cols(gh, gh)) + dot_t(f[:, :DH], g[:, DH:])
        s = jnp.where(causal, s, 0.0)
        sh, sl = split(s)
        ni[h] = dot(sh, v[...]) + dot(sl, v[...])
        dp[h] = fold(s)
        return 0

    lax.fori_loop(0, NS, stage_b, 0)

    def stage_c(s, total):
        @pl.when(s != me)
        def _():
            arrived(0, a_recv, s)

        c_send[s] = total
        return total + a_recv[s]

    lax.fori_loop(0, NS, stage_c, jnp.zeros((ROWS, DH), F32))

    def send_c(j, _):
        dst = lax.rem(me + j, NS)
        seq_copy(1, c_send.at[dst], c_recv, dst, me).start()
        return 0

    lax.fori_loop(1, NS, send_c, 0)
    c_recv[me] = c_send[me]

    power = p_send[...]
    for j in range(1, NH):
        power_copy(lax.rem(hd + j, NH), lax.rem(hd + j, NH)).wait_recv()
        power = power + p_recv[lax.rem(hd + j, NH)]
    power = power / (HEADS * DH) + 1e-05
    rp[...] = jnp.broadcast_to((1.0 / power).T[:, :1], (T, DH))

    def stage_d(j, _):
        h = lax.rem(me - j + NS, NS)

        @pl.when(j > 0)
        def _():
            arrived(1, c_recv, h)

        sh, sl = split(c_recv[h, :DH])
        key_total = c_recv[h, DH : DH + 1]
        f = qhl[h]
        w = jnp.concatenate([cols(sh, sh), cols(sl, sl)], axis=0)
        numer = ni[h] + fold(dot_t(f, w))
        qf = f[:, :DH].astype(F32) + f[:, DH:].astype(F32)
        den = jnp.sum(dp[h] + qf * key_total, axis=1, keepdims=True)
        rden = 1.0 / den
        student = numer * rden
        gn = (student - head_cols(t, h).astype(F32)) * rp[...] * rden
        gd = -jnp.sum(gn * student, axis=1, keepdims=True)
        ghl[h] = cols(*split(gn))
        gd_s[h] = jnp.broadcast_to(gd, (T, DH))
        th, tl = split(gn.T)
        d_send[h, :DH] = fold(dot(th, f) + dot(tl, f))
        d_send[h, DH:] = jnp.broadcast_to(jnp.sum(qf * gd, axis=0, keepdims=True), (8, DH))

        @pl.when(j > 0)
        def _():
            seq_copy(2, d_send.at[h], d_recv, h, me).start()

        return 0

    lax.fori_loop(0, NS, stage_d, 0)
    d_recv[me] = d_send[me]

    def map_grad(xt, feat, grad):
        r = feat * (grad - seg_sum(feat * grad))
        y = fold(dot(xt, cols(*split(r))))
        return (y[:, :FH] - y[:, FH:]).reshape(NS, 8, FH)

    def put(buf, h, g):
        @pl.when(lax.rem(h, 2) == 0)
        def _():
            buf[:, h // 2, :, :FH] = g

        @pl.when(lax.rem(h, 2) == 1)
        def _():
            buf[:, h // 2, :, FH:] = g

    def stage_e(h, _):
        g = ghl[h]
        gd = gd_s[h]
        f = qhl[h]
        b = jnp.where(causal, dot_t(g, vv[...]) + cols(gd, gd), 0.0)
        bh, bl = split(b)
        s = cols(*split(c_recv[h, :DH]))
        kf = khl[h]
        o = dot(bh, kf) + dot(bl, kf) + dot(g, jnp.concatenate([s, s], axis=0))
        grad = fold(o) + gd * c_recv[h, DH : DH + 1]
        qf = f[:, :DH].astype(F32) + f[:, DH:].astype(F32)
        put(gq_send, h, map_grad(head_cols(q, h).T, qf, grad))
        ni[h] = fold(dot(bh.T, f) + dot(bl.T, f))
        return 0

    lax.fori_loop(0, NS, stage_e, 0)
    gq_recv[me] = gq_send[me]

    def stage_f(j, total):
        s = NS - 1 - j

        @pl.when(s != me)
        def _():
            arrived(2, d_recv, s)

        f_send[s] = total
        return total + d_recv[s]

    lax.fori_loop(0, NS, stage_f, jnp.zeros((ROWS, DH), F32))

    def send_f(j, _):
        dst = lax.rem(me + j, NS)
        seq_copy(3, f_send.at[dst], f_recv, dst, me).start()
        return 0

    lax.fori_loop(1, NS, send_f, 0)
    f_recv[me] = f_send[me]

    def send_gq(j, _):
        dst = lax.rem(me + j, NS)
        seq_copy(4, gq_send.at[dst], gq_recv, dst, me).start()
        return 0

    lax.fori_loop(1, NS, send_gq, 0)

    def stage_g(j, _):
        h = lax.rem(me - j + NS, NS)

        @pl.when(j > 0)
        def _():
            arrived(3, f_recv, h)

        s = cols(*split(f_recv[h, :DH]))
        grad = ni[h] + fold(dot(v[...], s)) + f_recv[h, DH : DH + 1]
        f = khl[h]
        kf = f[:, :DH].astype(F32) + f[:, DH:].astype(F32)
        put(gk_send, h, map_grad(kt_s[...], kf, grad))
        return 0

    lax.fori_loop(0, NS, stage_g, 0)
    gk_recv[me] = gk_send[me]

    def send_gk(j, _):
        dst = lax.rem(me + j, NS)
        seq_copy(5, gk_send.at[dst], gk_recv, dst, me).start()
        return 0

    lax.fori_loop(1, NS, send_gk, 0)

    def collect(phase, buf, out):
        def step(s, total):
            @pl.when(s != me)
            def _():
                arrived(phase, buf, s)

            return total + buf[s]

        total = lax.fori_loop(0, NS, step, jnp.zeros((NS // 2, 8, DH), F32))
        for p in range(NS // 2):
            out[2 * p] = total[p, :, :FH]
            out[2 * p + 1] = total[p, :, FH:]

    collect(4, gq_recv, oq)
    collect(5, gk_recv, ok)

    for phase, buf, dst_buf in (
        (0, a_send, a_recv),
        (1, c_send, c_recv),
        (2, d_send, d_recv),
        (3, f_send, f_recv),
        (4, gq_send, gq_recv),
        (5, gk_send, gk_recv),
    ):
        def drain(j, _, phase=phase, buf=buf, dst_buf=dst_buf):
            dst = lax.rem(me + j, NS)
            seq_copy(phase, buf.at[dst], dst_buf, dst, me).wait_send()
            return 0

        lax.fori_loop(1, NS, drain, 0)
    for j in range(1, NH):
        power_copy(lax.rem(hd + j, NH), hd).wait_send()


def on_device(queries, keys, values, teacher, map_q, map_k):
    state = pltpu.VMEM((NS, ROWS, DH), F32)
    share = pltpu.VMEM((NS, NS // 2, 8, DH), F32)
    pair = pltpu.VMEM((NS, T, 2 * DH), BF16)
    whole = pltpu.VMEM((NS, T, DH), F32)
    vmem = pl.BlockSpec(memory_space=pltpu.VMEM)
    out = jax.ShapeDtypeStruct((NS, 8, FH), F32)
    return pl.pallas_call(
        kernel,
        out_shape=(out, out),
        in_specs=[vmem] * 6,
        out_specs=(vmem, vmem),
        scratch_shapes=[
            pair, pair, pair,
            whole, whole, whole,
            pltpu.VMEM((T, DH), F32),
            pltpu.VMEM((DH + 16, T), BF16),
            pltpu.VMEM((T, 2 * DH), BF16),
            pltpu.VMEM((DH, T), BF16),
            pltpu.VMEM((2 * DH, DH), BF16),
            pltpu.VMEM((8, T), F32),
            pltpu.VMEM((NH, 8, T), F32),
            state, state, state, state, state, state, state, state,
            share, share, share, share,
            pltpu.SemaphoreType.DMA((6, NS)),
            pltpu.SemaphoreType.DMA((6, NS)),
            pltpu.SemaphoreType.DMA((NH,)),
            pltpu.SemaphoreType.DMA((NH,)),
        ],
        compiler_params=pltpu.CompilerParams(
            collective_id=0, has_side_effects=True, vmem_limit_bytes=56 * 2**20
        ),
    )(queries, keys, values, teacher, map_q, map_k)


def solution(mesh):
    placed = (
        P("seq", "head"),
        P("seq", "head"),
        P("seq", "head"),
        P("seq", "head"),
        P("head", None, None),
        P("head", None, None),
    )
    return jax.shard_map(
        on_device,
        mesh=mesh,
        in_specs=placed,
        out_specs=(P("head", "seq", None), P("head", "seq", None)),
        check_vma=False,
    )
```

time: 281 us -> 107 us (0.38); the launches traced: 277 us -> 107 us
  waiting for transfers between devices: 102 us -> 0 us
  Pallas kernels: 0 us -> 101 us
  blocking collectives: 65.6 us -> 0 us
  matrix products: 46 us -> 0 us
  other arithmetic: 20.1 us -> 0 us
  between operations: 14.4 us -> 0.66 us
  local copies, waits for them, and re-layouts: 18.5 us -> 5.15 us
  starting transfers between devices: 11.1 us -> 0 us
    pallas_call x0 -> x1, Pallas kernels: none -> 101 us  [on_device(): pl.pallas_call(kernel, out_shape=(out, out), in_specs=[vmem] * 6, out_spe...]
    all_gather x4 -> x0, waiting for transfers between devices: 95.9 us -> none  [prefix_by_axis(): pieces = jax.tree.map(lambda part: lax.all_gather(part, axis), total)]
    all_gather x4 -> x0, blocking collectives: 50.4 us -> none  [prefix_by_axis(): pieces = jax.tree.map(lambda part: lax.all_gather(part, axis), total)]
    dot_general x16 -> x0, matrix products: 46 us -> none  [the longest x1 8.35 us: backward(): jnp.einsum('hqk,hqf->hkf', back_scores, q_cur, precision=exact_mode)]
    psum x1 -> x0, blocking collectives: 15.2 us -> none  [on_device(): power = lax.psum(local_power, 'head') / (HEADS * DH) + 1e-05]
    add x9 -> x0, other arithmetic: 11.4 us -> none  [the longest x7 11.4 us: add_pair(): return (earlier[0] + later[0], earlier[1] + later[1])]
    all_to_all x2 -> x0, starting transfers between devices: 10.9 us -> none  [summed_on_arrival(): lax.all_to_all(pieces, axis, split_axis=0, concat_axis=0, tiled=True)]
    unnamed x45 -> x8, local copies, waits for them, and re-layouts: 11.1 us -> 5.15 us
  transfers between devices with their start and end apart: 6 -> 0, of which waited for: 3 -> 0; matrix products, arithmetic and copies ran while one was open for 20% -> 0% of each run, Pallas kernels for 0% -> 0%
where the time goes in v1:
time: 107 us
  Pallas kernels  101 us (94%)
  local copies, waits for them, and re-layouts  5.15 us (5%)
    pallas_call x1, Pallas kernels, on_device(): pl.pallas_call(kernel, out_shape=(out, out), in_specs=[vmem] * 6, out_spe...  101 us
    unnamed x8, local copies, waits for them, and re-layouts  5.15 us

profile of v1, /device:TPU:0, one launch (start us, length us, event | category | flops | bytes accessed | tf_op | source)
XLA Modules:
  0.0 107.3 jit_solution(1826771622399504259)
XLA Ops:
  0.6 0.0 copy-start
  0.6 2.0 %copy.8.mq = bf16[16,128,64]{2,1,0:T(8,128)(2,1)} copy(bf16[16,128,64]{1,2,0:T(8,128)(2,1)} %param.10) | data formatting | bytes 524288 | tf_op args[4]
  2.6 0.0 copy-done
  2.6 1.0 copy.9.mk
  3.7 101.5 %shard_map.77 = (f32[16,8,64]{2,1,0:T(8,128)}, f32[16,8,64]{2,1,0:T(8,128)}) custom-call(bf16[256,2048]{1,0:T(8,128)(2,1)} %q.1, bf16[256,128]{1,0:T(8,128)(2,1)} %k.1, bf16[256,128]{1,0:T(8,128)(2,1)} %v.1, bf16[256,2048]{1,0:T(8,128)(2,1)} %t.1, bf16[16,128,64]{2,1,0:T(8,128)(2,1)} %copy.8.mq, bf16[16,128,64]{2,1,0:T(8,128)(2,1)} %copy.9.mk), custom_call_target="tpu_custom_call" | custom-call | tf_op jit(solution)/shard_map/pallas_call | solution.py:338
  105.1 0.0 copy-start.1
  105.1 1.5 %copy.12 = f32[16,8,64]{2,1,0:T(8,128)} copy(f32[16,8,64]{2,1,0:T(8,128)} %get-tuple-element.4) | data formatting | bytes 65536
  106.7 0.0 copy-done.1
  106.7 0.6 copy.13
Async XLA Ops:
  0.6 2.0 %copy-start = (bf16[16,128,64]{1,2,0:T(8,128)(2,1)S(1)}, bf16[16,128,64]{1,2,0:T(8,128)(2,1)}, u32[]{:S(2)}) copy-start(bf16[16,128,64]{1,2,0:T(8,128)(2,1)} %param.11) | copy-start | bytes 786436
  105.1 1.5 %copy-start.1 = (f32[16,8,64]{2,1,0:T(8,128)S(1)}, f32[16,8,64]{2,1,0:T(8,128)}, u32[]{:S(2)}) copy-start(f32[16,8,64]{2,1,0:T(8,128)} %get-tuple-element.5) | copy-start | bytes 98308

commit v2 on v1

v2 whole, which is shorter than its diff:
```python
import jax
import jax.numpy as jnp
from jax import lax
from jax.experimental import pallas as pl
from jax.experimental.pallas import tpu as pltpu
from jax.sharding import PartitionSpec as P

HEADS = 128
DH = 128
FH = 64
T = 256
NS = 16
NH = 8
HALF = DH // 2
ROWS = HALF + 8
SENT = HALF + 1
NG = 2
PG = NS // NG
GA, GB, GD, GE, GG = 4, 2, 2, 2, 2
MESH = pl.DeviceIdType.MESH
F32 = jnp.float32
BF16 = jnp.bfloat16


def split(x):
    high = x.astype(BF16)
    return high, (x - high.astype(F32)).astype(BF16)


def cols(x, y):
    return jnp.concatenate([x, y], axis=1)


def dot(a, b):
    return jnp.dot(a, b, preferred_element_type=F32)


def dot_t(a, b):
    return lax.dot_general(a, b, (((1,), (1,)), ((), ())), preferred_element_type=F32)


def join(x):
    return x[:, :DH].astype(F32) + x[:, DH:].astype(F32)


def fold(x):
    return x[:, :128] + x[:, 128:]


def kernel(
    q, k, v, t, mq, mk, oq, ok,
    khl, qhl, ghl, ni, dp, gd_s, rp, vta, vv, bb,
    p_send, p_recv, a_send, a_recv, c_send, c_recv, d_send, d_recv, f_send, f_recv,
    gq_send, gq_recv, gk_send, gk_recv, gk_sum,
    ss, rs, pss, prs,
):
    me = lax.axis_index("seq")
    hd = lax.axis_index("head")
    mine = me // 2
    sibling = me + 1 - 2 * lax.rem(me, 2)

    barrier = pltpu.get_barrier_semaphore()
    for j in range(1, NS):
        pl.semaphore_signal(
            barrier, inc=1, device_id={"seq": lax.rem(me + j, NS)}, device_id_type=MESH
        )
    for j in range(1, NH):
        pl.semaphore_signal(
            barrier, inc=1, device_id={"head": lax.rem(hd + j, NH)}, device_id_type=MESH
        )

    def sent(buf, g, slot):
        if buf.shape[2] == ROWS:
            return buf.at[g, slot, pl.ds(0, SENT)]
        return buf.at[g, slot]

    def seq_copy(phase, g, buf, dst_buf, dst):
        return pltpu.make_async_remote_copy(
            src_ref=sent(buf, g, dst),
            dst_ref=sent(dst_buf, g, me),
            send_sem=ss.at[phase, g, dst],
            recv_sem=rs.at[phase, g, me],
            device_id={"seq": dst},
            device_id_type=MESH,
        )

    def arrived(phase, g, buf, slot):
        pltpu.make_async_remote_copy(
            src_ref=sent(buf, g, slot),
            dst_ref=sent(buf, g, slot),
            send_sem=ss.at[phase, g, slot],
            recv_sem=rs.at[phase, g, slot],
            device_id={"seq": slot},
            device_id_type=MESH,
        ).wait_recv()

    def send_all(phase, g, buf, dst_buf):
        def step(j, _):
            seq_copy(phase, g, buf, dst_buf, lax.rem(me + j, NS)).start()
            return 0

        lax.fori_loop(1, NS, step, 0)

    def owners(cs, own):
        return [2 * c + i for c in (cs[:-1] if own else cs) for i in range(2)] + (
            [sibling] if own else []
        )

    def states(buf, g, c):
        return jnp.concatenate([buf[g, 2 * c, :HALF], buf[g, 2 * c + 1, :HALF]], axis=0)

    def totals(buf, g, c):
        return buf[g, 2 * c, HALF:SENT]

    def power_copy(dst, slot):
        return pltpu.make_async_remote_copy(
            src_ref=p_send,
            dst_ref=p_recv.at[slot],
            send_sem=pss.at[dst],
            recv_sem=prs.at[slot],
            device_id={"head": dst},
            device_id_type=MESH,
        )

    def head_cols(ref, h):
        return ref[:, pl.ds(pl.multiple_of(h * DH, DH), DH)]

    even = lax.broadcasted_iota(jnp.int32, (DH, DH), 1) < FH

    row = lax.broadcasted_iota(jnp.int32, (2 * DH, DH), 0)
    col = lax.broadcasted_iota(jnp.int32, (2 * DH, DH), 1)
    bb[...] = jnp.where(lax.rem(row, DH) // FH == col // FH, 1.0, 0.0).astype(BF16)
    vta[:DH] = v[...].T
    vta[DH:] = jnp.ones((16, T), BF16)
    vv[...] = cols(v[...], v[...])

    tri = lax.broadcasted_iota(jnp.int32, (DH, DH), 0) >= lax.broadcasted_iota(
        jnp.int32, (DH, DH), 1
    )

    def seg_sum(x):
        return dot(cols(*split(x)), bb[...])

    def features(xs, ms):
        es = [jnp.exp(dot_t(x, jnp.concatenate([m, -m], axis=0))) for x, m in zip(xs, ms)]
        sums = [seg_sum(e) for e in es]
        return [cols(*split(e * (1.0 / z))) for e, z in zip(es, sums)]

    def stage_a(g, j0, own):
        cs = [lax.rem(mine + 1 + j0 + i, PG) for i in range(GA)]
        hs = [g * PG + c for c in cs]
        fs = features([k[...]] * GA, [mk[h] for h in hs])
        ps = [fold(dot(vta[...], f)) for f in fs]
        for c, h, f, p in zip(cs, hs, fs, ps):
            khl[h] = f
            a_send[g, 2 * c, :HALF] = p[:HALF]
            a_send[g, 2 * c + 1, :HALF] = p[HALF:DH]
            a_send[g, 2 * c, HALF:] = p[DH : DH + 8]
            a_send[g, 2 * c + 1, HALF:] = p[DH : DH + 8]
        return owners(cs, own)

    for g in range(NG):
        for j0 in range(0, PG, GA):
            dsts = stage_a(g, j0, j0 + GA == PG)
            if g == 0 and j0 == 0:
                pl.semaphore_wait(barrier, NS + NH - 2)
            for dst in dsts:
                seq_copy(0, g, a_send, a_recv, dst).start()
        a_recv[g, me] = a_send[g, me]

    def squares(j, total):
        x = head_cols(t, j).astype(F32)
        return total + x * x

    sq = lax.fori_loop(0, NS, squares, jnp.zeros((T, DH), F32))
    p_send[...] = jnp.broadcast_to(jnp.sum(sq.T, axis=0, keepdims=True), (8, T))
    for j in range(1, NH):
        power_copy(lax.rem(hd + j, NH), hd).start()

    def lower(x, y, z):
        return jnp.concatenate([cols(x, jnp.zeros_like(x)), cols(y, z)], axis=0)

    def stage_b(g, _):
        hs = [g * GB + i for i in range(GB)]
        fs = features([head_cols(q, h) for h in hs], [mq[h] for h in hs])
        gs = [khl[h] for h in hs]
        ss_ = [
            dot_t(f, cols(g[:, :DH], g[:, :DH])) + dot_t(f[:, :DH], g[:, DH:])
            for f, g in zip(fs, gs)
        ]
        for h, f, s in zip(hs, fs, ss_):
            x = jnp.where(tri, s[:DH, :DH], 0.0)
            y = s[DH:, :DH]
            z = jnp.where(tri, s[DH:, DH:], 0.0)
            (xh, xl), (yh, yl), (zh, zl) = split(x), split(y), split(z)
            ni[h] = dot(lower(xh, yh, zh), v[...]) + dot(lower(xl, yl, zl), v[...])
            dp[h, :DH] = x
            dp[h, DH:] = y + z
            qhl[h] = f
        return 0

    lax.fori_loop(0, NS // GB, stage_b, 0)

    def scan(phase, g, source, send, back, reverse):
        def step(j, total):
            s = NS - 1 - j if reverse else j

            @pl.when(s != me)
            def _():
                arrived(phase, g, source, s)

            send[g, s] = total
            return total + source[g, s]

        lax.fori_loop(0, NS, step, jnp.zeros((ROWS, DH), F32))
        send_all(phase + 1, g, send, back)
        back[g, me] = send[g, me]

    for g in range(NG):
        scan(0, g, a_recv, c_send, c_recv, False)

    power = p_send[...]
    for j in range(1, NH):
        power_copy(lax.rem(hd + j, NH), lax.rem(hd + j, NH)).wait_recv()
        power = power + p_recv[lax.rem(hd + j, NH)]
    power = power / (HEADS * DH) + 1e-05
    rp[...] = jnp.broadcast_to((1.0 / power).T[:, :1], (T, DH))

    def stage_d(g, cs, own):
        hs = [g * PG + c for c in cs]
        dsts = owners(cs, own)
        for o in dsts:
            arrived(1, g, c_recv, o)
        fs = [qhl[h] for h in hs]
        ws = []
        for c in cs:
            sh, sl = split(states(c_recv, g, c))
            ws.append(jnp.concatenate([cols(sh, sh), cols(sl, sl)], axis=0))
        numers = [ni[h] + fold(dot_t(f, w)) for h, f, w in zip(hs, fs, ws)]
        qfs = [join(f) for f in fs]
        dens = [
            jnp.sum(dp[h] + qf * totals(c_recv, g, c), axis=1, keepdims=True)
            for h, qf, c in zip(hs, qfs, cs)
        ]
        rdens = [1.0 / den for den in dens]
        students = [numer * rden for numer, rden in zip(numers, rdens)]
        gns = [
            (student - head_cols(t, h).astype(F32)) * rp[...] * rden
            for h, student, rden in zip(hs, students, rdens)
        ]
        gds = [-jnp.sum(gn * st, axis=1, keepdims=True) for gn, st in zip(gns, students)]
        ts = [split(gn.T) for gn in gns]
        outs = [fold(dot(th, f) + dot(tl, f)) for (th, tl), f in zip(ts, fs)]
        for c, h, qf, gn, gd, out in zip(cs, hs, qfs, gns, gds, outs):
            total = jnp.broadcast_to(jnp.sum(qf * gd, axis=0, keepdims=True), (8, DH))
            d_send[g, 2 * c, :HALF] = out[:HALF]
            d_send[g, 2 * c + 1, :HALF] = out[HALF:]
            d_send[g, 2 * c, HALF:] = total
            d_send[g, 2 * c + 1, HALF:] = total
            ghl[h] = cols(*split(gn))
            gd_s[h] = jnp.broadcast_to(gd, (T, DH))
        for o in dsts:
            seq_copy(2, g, d_send, d_recv, o).start()

    def rotated(stage, g, size):
        def heads(j0):
            return [lax.rem(mine - j0 - i + PG, PG) for i in range(size)][::-1]

        def step(j, _):
            stage(g, heads(j * size), False)
            return 0

        stage(g, heads(0), True)
        lax.fori_loop(1, PG // size, step, 0)

    def map_grads(xts, feats, grads):
        rs_ = [f * g for f, g in zip(feats, grads)]
        rs_ = [r - f * seg_sum(r) for r, f in zip(rs_, feats)]
        ys = [fold(dot(xt, cols(*split(r)))) for xt, r in zip(xts, rs_)]
        return [y - pltpu.roll(y, FH, 1) for y in ys]

    def stage_e(group, p):
        cs = [p * GE + i for i in range(GE)]
        hs = [group * PG + c for c in cs]
        gs = [ghl[h] for h in hs]
        bs = [dot_t(g, vv[...]) for g in gs]
        lows = []
        for h, b in zip(hs, bs):
            gd = gd_s[h]
            x = jnp.where(tri, b[:DH, :DH] + gd[:DH], 0.0)
            y = b[DH:, :DH] + gd[DH:]
            z = jnp.where(tri, b[DH:, DH:] + gd[DH:], 0.0)
            lows.append((split(x), split(y), split(z)))
        grads = []
        for c, h, g, (x, y, z) in zip(cs, hs, gs, lows):
            s = cols(*split(states(c_recv, group, c)))
            kf = khl[h]
            o = dot(g, jnp.concatenate([s, s], axis=0))
            o = o + dot(lower(x[0], y[0], z[0]), kf) + dot(lower(x[1], y[1], z[1]), kf)
            grads.append(fold(o) + gd_s[h] * totals(c_recv, group, c))
        fs = [qhl[h] for h in hs]
        outs = map_grads([head_cols(q, h).T for h in hs], [join(f) for f in fs], grads)
        for h, f, (x, y, z) in zip(hs, fs, lows):
            o = [
                dot(
                    jnp.concatenate(
                        [cols(x[i].T, y[i].T), cols(jnp.zeros_like(x[i]), z[i].T)], axis=0
                    ),
                    f,
                )
                for i in range(2)
            ]
            ni[h] = fold(o[0] + o[1])
        for i in range(0, GE, 2):
            both = jnp.where(even, outs[i], -outs[i + 1])
            gq_send[group, :, p * (GE // 2) + i // 2] = both.reshape(NS, 8, DH)

    for g in range(NG):
        rotated(stage_d, g, GD)
        d_recv[g, me] = d_send[g, me]

        def step_e(p, _, g=g):
            stage_e(g, p)
            return 0

        lax.fori_loop(0, PG // GE, step_e, 0)
        gq_recv[g, me] = gq_send[g, me]

    for g in range(NG):
        scan(2, g, d_recv, f_send, f_recv, True)
    for g in range(NG):
        send_all(4, g, gq_send, gq_recv)

    def stage_g(g, cs, own):
        hs = [g * PG + c for c in cs]
        for o in owners(cs, own):
            arrived(3, g, f_recv, o)
        ss_ = [cols(*split(states(f_recv, g, c))) for c in cs]
        grads = [
            ni[h] + fold(dot(v[...], s)) + totals(f_recv, g, c)
            for c, h, s in zip(cs, hs, ss_)
        ]
        outs = map_grads([k[...].T] * GG, [join(khl[h]) for h in hs], grads)
        for c, out in zip(cs, outs):
            odd = lax.rem(c, 2)
            sign = (1 - 2 * odd).astype(F32)
            own_half = jnp.where(even == (odd == 0), out * sign, 0.0)
            gk_sum[g, c // 2] += own_half

    gk_sum[...] = jnp.zeros_like(gk_sum)
    for g in range(NG):
        rotated(stage_g, g, GG)
        for p in range(PG // 2):
            gk_send[g, :, p] = gk_sum[g, p].reshape(NS, 8, DH)
        gk_recv[g, me] = gk_send[g, me]
        send_all(5, g, gk_send, gk_recv)

    def collect(phase, g, buf, out):
        def step(s, total):
            @pl.when(s != me)
            def _():
                arrived(phase, g, buf, s)

            return total + buf[g, s]

        total = lax.fori_loop(0, NS, step, jnp.zeros((PG // 2, 8, DH), F32))
        for p in range(PG // 2):
            out[g * PG + 2 * p] = total[p, :, :FH]
            out[g * PG + 2 * p + 1] = total[p, :, FH:]

    for g in range(NG):
        collect(4, g, gq_recv, oq)
    for g in range(NG):
        collect(5, g, gk_recv, ok)

    for phase, buf, dst_buf in (
        (0, a_send, a_recv),
        (1, c_send, c_recv),
        (2, d_send, d_recv),
        (3, f_send, f_recv),
        (4, gq_send, gq_recv),
        (5, gk_send, gk_recv),
    ):
        def drain(j, _, phase=phase, buf=buf, dst_buf=dst_buf):
            for g in range(NG):
                seq_copy(phase, g, buf, dst_buf, lax.rem(me + j, NS)).wait_send()
            return 0

        lax.fori_loop(1, NS, drain, 0)
    for j in range(1, NH):
        power_copy(lax.rem(hd + j, NH), hd).wait_send()


def on_device(queries, keys, values, teacher, map_q, map_k):
    state = pltpu.VMEM((NG, NS, ROWS, DH), F32)
    share = pltpu.VMEM((NG, NS, PG // 2, 8, DH), F32)
    pair = pltpu.VMEM((NS, T, 2 * DH), BF16)
    whole = pltpu.VMEM((NS, T, DH), F32)
    vmem = pl.BlockSpec(memory_space=pltpu.VMEM)
    out = jax.ShapeDtypeStruct((NS, 8, FH), F32)
    return pl.pallas_call(
        kernel,
        out_shape=(out, out),
        in_specs=[vmem] * 6,
        out_specs=(vmem, vmem),
        scratch_shapes=[
            pair, pair, pair,
            whole, whole, whole,
            pltpu.VMEM((T, DH), F32),
            pltpu.VMEM((DH + 16, T), BF16),
            pltpu.VMEM((T, 2 * DH), BF16),
            pltpu.VMEM((2 * DH, DH), BF16),
            pltpu.VMEM((8, T), F32),
            pltpu.VMEM((NH, 8, T), F32),
            state, state, state, state, state, state, state, state,
            share, share, share, share,
            pltpu.VMEM((NG, PG // 2, DH, DH), F32),
            pltpu.SemaphoreType.DMA((6, NG, NS)),
            pltpu.SemaphoreType.DMA((6, NG, NS)),
            pltpu.SemaphoreType.DMA((NH,)),
            pltpu.SemaphoreType.DMA((NH,)),
        ],
        compiler_params=pltpu.CompilerParams(
            collective_id=0, has_side_effects=True, vmem_limit_bytes=56 * 2**20
        ),
    )(queries, keys, values, teacher, map_q.swapaxes(1, 2), map_k.swapaxes(1, 2))


def solution(mesh):
    placed = (
        P("seq", "head"),
        P("seq", "head"),
        P("seq", "head"),
        P("seq", "head"),
        P("head", None, None),
        P("head", None, None),
    )
    return jax.shard_map(
        on_device,
        mesh=mesh,
        in_specs=placed,
        out_specs=(P("head", "seq", None), P("head", "seq", None)),
        check_vma=False,
    )
```

time: 107 us -> 79.4 us (0.74)
  Pallas kernels: 101 us -> 75.9 us
  local copies, waits for them, and re-layouts: 5.15 us -> 2.14 us
    pallas_call x1, Pallas kernels: 101 us -> 75.9 us  [on_device(): pl.pallas_call(kernel, out_shape=(out, out), in_specs=[vmem] * 6, out_spe...]
    unnamed x8 -> x4, local copies, waits for them, and re-layouts: 5.15 us -> 2.14 us
where the time goes in v2:
time: 79.4 us; the launch traced here: 78.7 us
  Pallas kernels  75.9 us (96%)
  local copies, waits for them, and re-layouts  2.14 us (3%)
    pallas_call x1, Pallas kernels, on_device(): pl.pallas_call(kernel, out_shape=(out, out), in_specs=[vmem] * 6, out_spe...  75.9 us
    unnamed x4, local copies, waits for them, and re-layouts  2.14 us

profile of v2, /device:TPU:0, one launch (start us, length us, event | category | flops | bytes accessed | tf_op | source)
XLA Modules:
  0.0 78.7 jit_solution(15639035766788971145)
XLA Ops:
  0.6 75.9 %shard_map.77 = (f32[16,8,64]{2,1,0:T(8,128)}, f32[16,8,64]{2,1,0:T(8,128)}) custom-call(bf16[256,2048]{1,0:T(8,128)(2,1)} %q.1, bf16[256,128]{1,0:T(8,128)(2,1)} %k.1, bf16[256,128]{1,0:T(8,128)(2,1)} %v.1, bf16[256,2048]{1,0:T(8,128)(2,1)} %t.1, bf16[16,64,128]{2,1,0:T(8,128)(2,1)} %bitcast.2, bf16[16,64,128]{2,1,0:T(8,128)(2,1)} %bitcast.3), custom_call_target="tpu_custom_call" | custom-call | tf_op jit(solution)/shard_map/pallas_call | solution.py:401
  76.5 0.0 copy-start
  76.5 1.5 %copy.10 = f32[16,8,64]{2,1,0:T(8,128)} copy(f32[16,8,64]{2,1,0:T(8,128)} %get-tuple-element.4) | data formatting | bytes 65536
  78.0 0.0 copy-done
  78.1 0.6 copy.11
Async XLA Ops:
  76.5 1.5 %copy-start = (f32[16,8,64]{2,1,0:T(8,128)S(1)}, f32[16,8,64]{2,1,0:T(8,128)}, u32[]{:S(2)}) copy-start(f32[16,8,64]{2,1,0:T(8,128)} %get-tuple-element.5) | copy-start | bytes 98308

commit v3 on v2

--- a/solution.py
+++ b/solution.py
@@ -11,12 +11,13 @@
 T = 256
 NS = 16
 NH = 8
-HALF = DH // 2
-ROWS = HALF + 8
-SENT = HALF + 1
 NG = 2
 PG = NS // NG
-GA, GB, GD, GE, GG = 4, 2, 2, 2, 2
+NO = NS // PG
+PART = DH // NO
+ROWS = PART + 8
+SENT = PART + 1
+GA, GB, GD, GE, GG = 4, 4, 2, 4, 2
 MESH = pl.DeviceIdType.MESH
 F32 = jnp.float32
 BF16 = jnp.bfloat16
@@ -48,7 +49,8 @@
 
 
 def kernel(
-    q, k, v, t, mq, mk, oq, ok,
+    q_in, k, v, t_in, mq_in, mk, oq, ok,
+    q, t, mq, in_sem,
     khl, qhl, ghl, ni, dp, gd_s, rp, vta, vv, bb,
     p_send, p_recv, a_send, a_recv, c_send, c_recv, d_send, d_recv, f_send, f_recv,
     gq_send, gq_recv, gk_send, gk_recv, gk_sum,
@@ -56,8 +58,15 @@
 ):
     me = lax.axis_index("seq")
     hd = lax.axis_index("head")
-    mine = me // 2
-    sibling = me + 1 - 2 * lax.rem(me, 2)
+    mine = me // NO
+    siblings = [mine * NO + lax.rem(me + i, NO) for i in range(1, NO)]
+
+    loads = [
+        pltpu.make_async_copy(src, dst, in_sem.at[i])
+        for i, (src, dst) in enumerate(((t_in, t), (q_in, q), (mq_in, mq)))
+    ]
+    for load in loads:
+        load.start()
 
     barrier = pltpu.get_barrier_semaphore()
     for j in range(1, NS):
@@ -102,15 +111,20 @@
         lax.fori_loop(1, NS, step, 0)
 
     def owners(cs, own):
-        return [2 * c + i for c in (cs[:-1] if own else cs) for i in range(2)] + (
-            [sibling] if own else []
+        return [NO * c + i for c in (cs[:-1] if own else cs) for i in range(NO)] + (
+            siblings if own else []
         )
 
     def states(buf, g, c):
-        return jnp.concatenate([buf[g, 2 * c, :HALF], buf[g, 2 * c + 1, :HALF]], axis=0)
+        return jnp.concatenate([buf[g, NO * c + i, :PART] for i in range(NO)], axis=0)
 
     def totals(buf, g, c):
-        return buf[g, 2 * c, HALF:SENT]
+        return buf[g, NO * c, PART:SENT]
+
+    def put_state(buf, g, c, state, total):
+        for i in range(NO):
+            buf[g, NO * c + i, :PART] = state[i * PART : (i + 1) * PART]
+            buf[g, NO * c + i, PART:] = total
 
     def power_copy(dst, slot):
         return pltpu.make_async_remote_copy(
@@ -153,10 +167,7 @@
         ps = [fold(dot(vta[...], f)) for f in fs]
         for c, h, f, p in zip(cs, hs, fs, ps):
             khl[h] = f
-            a_send[g, 2 * c, :HALF] = p[:HALF]
-            a_send[g, 2 * c + 1, :HALF] = p[HALF:DH]
-            a_send[g, 2 * c, HALF:] = p[DH : DH + 8]
-            a_send[g, 2 * c + 1, HALF:] = p[DH : DH + 8]
+            put_state(a_send, g, c, p[:DH], p[DH : DH + 8])
         return owners(cs, own)
 
     for g in range(NG):
@@ -167,6 +178,9 @@
             for dst in dsts:
                 seq_copy(0, g, a_send, a_recv, dst).start()
         a_recv[g, me] = a_send[g, me]
+
+    for load in loads:
+        load.wait()
 
     def squares(j, total):
         x = head_cols(t, j).astype(F32)
@@ -253,10 +267,7 @@
         outs = [fold(dot(th, f) + dot(tl, f)) for (th, tl), f in zip(ts, fs)]
         for c, h, qf, gn, gd, out in zip(cs, hs, qfs, gns, gds, outs):
             total = jnp.broadcast_to(jnp.sum(qf * gd, axis=0, keepdims=True), (8, DH))
-            d_send[g, 2 * c, :HALF] = out[:HALF]
-            d_send[g, 2 * c + 1, :HALF] = out[HALF:]
-            d_send[g, 2 * c, HALF:] = total
-            d_send[g, 2 * c + 1, HALF:] = total
+            put_state(d_send, g, c, out, total)
             ghl[h] = cols(*split(gn))
             gd_s[h] = jnp.broadcast_to(gd, (T, DH))
         for o in dsts:
@@ -315,22 +326,32 @@
             both = jnp.where(even, outs[i], -outs[i + 1])
             gq_send[group, :, p * (GE // 2) + i // 2] = both.reshape(NS, 8, DH)
 
-    for g in range(NG):
+    def run_d(g):
         rotated(stage_d, g, GD)
         d_recv[g, me] = d_send[g, me]
 
-        def step_e(p, _, g=g):
+    def run_e(g):
+        def step_e(p, _):
             stage_e(g, p)
             return 0
 
         lax.fori_loop(0, PG // GE, step_e, 0)
         gq_recv[g, me] = gq_send[g, me]
 
-    for g in range(NG):
+    def run_f(g):
         scan(2, g, d_recv, f_send, f_recv, True)
-    for g in range(NG):
+
+    def run_q(g):
         send_all(4, g, gq_send, gq_recv)
 
+    run_d(0)
+    run_d(1)
+    run_e(0)
+    run_f(0)
+    run_e(1)
+    run_f(1)
+    run_q(0)
+    run_q(1)
     def stage_g(g, cs, own):
         hs = [g * PG + c for c in cs]
         for o in owners(cs, own):
@@ -364,9 +385,7 @@
             return total + buf[g, s]
 
         total = lax.fori_loop(0, NS, step, jnp.zeros((PG // 2, 8, DH), F32))
-        for p in range(PG // 2):
-            out[g * PG + 2 * p] = total[p, :, :FH]
-            out[g * PG + 2 * p + 1] = total[p, :, FH:]
+        out[pl.ds(g * (PG // 2), PG // 2)] = total
 
     for g in range(NG):
         collect(4, g, gq_recv, oq)
@@ -391,19 +410,32 @@
         power_copy(lax.rem(hd + j, NH), hd).wait_send()
 
 
+def unpack(pq, pk, oq, ok):
+    for packed, out in ((pq, oq), (pk, ok)):
+        for p in range(NS // 2):
+            x = packed[p]
+            out[2 * p] = x[:, :FH]
+            out[2 * p + 1] = x[:, FH:]
+
+
 def on_device(queries, keys, values, teacher, map_q, map_k):
     state = pltpu.VMEM((NG, NS, ROWS, DH), F32)
     share = pltpu.VMEM((NG, NS, PG // 2, 8, DH), F32)
     pair = pltpu.VMEM((NS, T, 2 * DH), BF16)
     whole = pltpu.VMEM((NS, T, DH), F32)
     vmem = pl.BlockSpec(memory_space=pltpu.VMEM)
-    out = jax.ShapeDtypeStruct((NS, 8, FH), F32)
-    return pl.pallas_call(
+    hbm = pl.BlockSpec(memory_space=pl.ANY)
+    out = jax.ShapeDtypeStruct((NS // 2, 8, DH), F32)
+    packed = pl.pallas_call(
         kernel,
         out_shape=(out, out),
-        in_specs=[vmem] * 6,
+        in_specs=[hbm, vmem, vmem, hbm, hbm, vmem],
         out_specs=(vmem, vmem),
         scratch_shapes=[
+            pltpu.VMEM((T, NS * DH), BF16),
+            pltpu.VMEM((T, NS * DH), BF16),
+            pltpu.VMEM((NS, FH, DH), BF16),
+            pltpu.SemaphoreType.DMA((3,)),
             pair, pair, pair,
             whole, whole, whole,
             pltpu.VMEM((T, DH), F32),
@@ -425,6 +457,9 @@
         ),
     )(queries, keys, values, teacher, map_q.swapaxes(1, 2), map_k.swapaxes(1, 2))
 
+    final = jax.ShapeDtypeStruct((NS, 8, FH), F32)
+    return pl.pallas_call(unpack, out_shape=(final, final))(*packed)
+
 
 def solution(mesh):
     placed = (

time: 79.4 us -> 77 us (0.970)
  local copies, waits for them, and re-layouts: 2.14 us -> 0 us
    unnamed x4 -> x0, local copies, waits for them, and re-layouts: 2.14 us -> none
    pallas_call x1 -> x2, Pallas kernels: 75.9 us -> 76.2 us  [the longest x1 74.7 us: on_device(): pl.pallas_call(kernel, out_shape=(out, out), in_specs=[hbm, vmem, vmem, h...]
where the time goes in v3:
time: 77 us; the launch traced here: 76.9 us
  Pallas kernels  76.2 us (99%)
    pallas_call x1, Pallas kernels, on_device(): pl.pallas_call(kernel, out_shape=(out, out), in_specs=[hbm, vmem, vmem, h...  74.7 us

profile of v3, /device:TPU:0, one launch (start us, length us, event | category | flops | bytes accessed | tf_op | source)
XLA Modules:
  0.0 76.9 jit_solution(17596139584843283858)
XLA Ops:
  0.6 74.7 %shard_map.77 = (f32[8,8,128]{2,1,0:T(8,128)}, f32[8,8,128]{2,1,0:T(8,128)}) custom-call(bf16[256,2048]{1,0:T(8,128)(2,1)} %q_in.1, bf16[256,128]{1,0:T(8,128)(2,1)} %k.1, bf16[256,128]{1,0:T(8,128)(2,1)} %v.1, bf16[256,2048]{1,0:T(8,128)(2,1)} %t_in.1, bf16[16,64,128]{2,1,0:T(8,128)(2,1)} %bitcast.2, bf16[16,64,128]{2,1,0:T(8,128)(2,1)} %bitcast.3), custom_call_target="tpu_custom_call" | custom-call | tf_op jit(solution)/shard_map/pallas_call | solution.py:429
  75.3 1.5 %shard_map.78 = (f32[16,8,64]{2,1,0:T(8,128)}, f32[16,8,64]{2,1,0:T(8,128)}) custom-call(f32[8,8,128]{2,1,0:T(8,128)} %get-tuple-element.4.pq, f32[8,8,128]{2,1,0:T(8,128)} %get-tuple-element.5.pk), custom_call_target="tpu_custom_call" | custom-call | tf_op jit(solution)/shard_map/pallas_call | solution.py:461

commit v4 on v3

--- a/solution.py
+++ b/solution.py
@@ -17,7 +17,7 @@
 PART = DH // NO
 ROWS = PART + 8
 SENT = PART + 1
-GA, GB, GD, GE, GG = 4, 4, 2, 4, 2
+GA, GB, GD, GE, GG = 4, 4, 2, 4, 4
 MESH = pl.DeviceIdType.MESH
 F32 = jnp.float32
 BF16 = jnp.bfloat16
@@ -49,8 +49,8 @@
 
 
 def kernel(
-    q_in, k, v, t_in, mq_in, mk, oq, ok,
-    q, t, mq, in_sem,
+    q_in, k_in, v_in, t_in, mq_in, mk_in, oq, ok,
+    q, t, mq, k, v, mk, in_sem,
     khl, qhl, ghl, ni, dp, gd_s, rp, vta, vv, bb,
     p_send, p_recv, a_send, a_recv, c_send, c_recv, d_send, d_recv, f_send, f_recv,
     gq_send, gq_recv, gk_send, gk_recv, gk_sum,
@@ -63,7 +63,9 @@
 
     loads = [
         pltpu.make_async_copy(src, dst, in_sem.at[i])
-        for i, (src, dst) in enumerate(((t_in, t), (q_in, q), (mq_in, mq)))
+        for i, (src, dst) in enumerate(
+            ((k_in, k), (mk_in, mk), (v_in, v), (t_in, t), (q_in, q), (mq_in, mq))
+        )
     ]
     for load in loads:
         load.start()
@@ -104,6 +106,13 @@
         ).wait_recv()
 
     def send_all(phase, g, buf, dst_buf):
+        if phase >= 4:
+            hops = sorted(range(1, NS), key=lambda i: -min(i // 4, 4 - i // 4) - min(i % 4, 4 - i % 4))
+            for i in hops:
+                y, x = lax.rem(me // 4 + i // 4, 4), lax.rem(me + i, 4)
+                seq_copy(phase, g, buf, dst_buf, 4 * y + x).start()
+            return
+
         def step(j, _):
             seq_copy(phase, g, buf, dst_buf, lax.rem(me + j, NS)).start()
             return 0
@@ -144,6 +153,8 @@
     row = lax.broadcasted_iota(jnp.int32, (2 * DH, DH), 0)
     col = lax.broadcasted_iota(jnp.int32, (2 * DH, DH), 1)
     bb[...] = jnp.where(lax.rem(row, DH) // FH == col // FH, 1.0, 0.0).astype(BF16)
+    for load in loads[:3]:
+        load.wait()
     vta[:DH] = v[...].T
     vta[DH:] = jnp.ones((16, T), BF16)
     vv[...] = cols(v[...], v[...])
@@ -179,7 +190,7 @@
                 seq_copy(0, g, a_send, a_recv, dst).start()
         a_recv[g, me] = a_send[g, me]
 
-    for load in loads:
+    for load in loads[3:]:
         load.wait()
 
     def squares(j, total):
@@ -429,13 +440,16 @@
     packed = pl.pallas_call(
         kernel,
         out_shape=(out, out),
-        in_specs=[hbm, vmem, vmem, hbm, hbm, vmem],
+        in_specs=[hbm] * 6,
         out_specs=(vmem, vmem),
         scratch_shapes=[
             pltpu.VMEM((T, NS * DH), BF16),
             pltpu.VMEM((T, NS * DH), BF16),
             pltpu.VMEM((NS, FH, DH), BF16),
-            pltpu.SemaphoreType.DMA((3,)),
+            pltpu.VMEM((T, DH), BF16),
+            pltpu.VMEM((T, DH), BF16),
+            pltpu.VMEM((NS, FH, DH), BF16),
+            pltpu.SemaphoreType.DMA((6,)),
             pair, pair, pair,
             whole, whole, whole,
             pltpu.VMEM((T, DH), F32),

time: 77 us -> 76.1 us (0.988)
  Pallas kernels: 76.2 us -> 75.1 us
    pallas_call x1, Pallas kernels: 74.7 us -> 73.6 us  [on_device(): pl.pallas_call(kernel, out_shape=(out, out), in_specs=[hbm] * 6, out_spec...]
where the time goes in v4:
time: 76.1 us; the launch traced here: 75.8 us
  Pallas kernels  75.1 us (99%)
    pallas_call x1, Pallas kernels, on_device(): pl.pallas_call(kernel, out_shape=(out, out), in_specs=[hbm] * 6, out_spec...  73.6 us

profile of v4, /device:TPU:0, one launch (start us, length us, event | category | flops | bytes accessed | tf_op | source)
XLA Modules:
  0.0 75.8 jit_solution(6123257110917968630)
XLA Ops:
  0.6 73.6 %shard_map.77 = (f32[8,8,128]{2,1,0:T(8,128)}, f32[8,8,128]{2,1,0:T(8,128)}) custom-call(bf16[256,2048]{1,0:T(8,128)(2,1)} %q_in.1, bf16[256,128]{1,0:T(8,128)(2,1)} %k_in.1, bf16[256,128]{1,0:T(8,128)(2,1)} %v_in.1, bf16[256,2048]{1,0:T(8,128)(2,1)} %t_in.1, bf16[16,64,128]{2,1,0:T(8,128)(2,1)} %bitcast.2, bf16[16,64,128]{2,1,0:T(8,128)(2,1)} %bitcast.3), custom_call_target="tpu_custom_call" | custom-call | tf_op jit(solution)/shard_map/pallas_call | solution.py:440
  74.3 1.5 %shard_map.78 = (f32[16,8,64]{2,1,0:T(8,128)}, f32[16,8,64]{2,1,0:T(8,128)}) custom-call(f32[8,8,128]{2,1,0:T(8,128)} %get-tuple-element.4.pq, f32[8,8,128]{2,1,0:T(8,128)} %get-tuple-element.5.pk), custom_call_target="tpu_custom_call" | custom-call | tf_op jit(solution)/shard_map/pallas_call | solution.py:475

commit v5 on v4

--- a/solution.py
+++ b/solution.py
@@ -17,7 +17,7 @@
 PART = DH // NO
 ROWS = PART + 8
 SENT = PART + 1
-GA, GB, GD, GE, GG = 4, 4, 2, 4, 4
+GA, GB, GD, GE, GG = 2, 4, 2, 4, 4
 MESH = pl.DeviceIdType.MESH
 F32 = jnp.float32
 BF16 = jnp.bfloat16

time: 76.1 us -> 76.9 us (1.011)
  Pallas kernels: 75.1 us -> 76 us
    pallas_call x1, Pallas kernels: 73.6 us -> 74.5 us  [on_device(): pl.pallas_call(kernel, out_shape=(out, out), in_specs=[hbm] * 6, out_spec...]
where the time goes in v5:
time: 76.9 us; the launch traced here: 76.7 us
  Pallas kernels  76 us (99%)
    pallas_call x1, Pallas kernels, on_device(): pl.pallas_call(kernel, out_shape=(out, out), in_specs=[hbm] * 6, out_spec...  74.5 us

profile of v5, /device:TPU:0, one launch (start us, length us, event | category | flops | bytes accessed | tf_op | source)
XLA Modules:
  0.0 76.7 jit_solution(9968677756291714617)
XLA Ops:
  0.6 74.5 %shard_map.77 = (f32[8,8,128]{2,1,0:T(8,128)}, f32[8,8,128]{2,1,0:T(8,128)}) custom-call(bf16[256,2048]{1,0:T(8,128)(2,1)} %q_in.1, bf16[256,128]{1,0:T(8,128)(2,1)} %k_in.1, bf16[256,128]{1,0:T(8,128)(2,1)} %v_in.1, bf16[256,2048]{1,0:T(8,128)(2,1)} %t_in.1, bf16[16,64,128]{2,1,0:T(8,128)(2,1)} %bitcast.2, bf16[16,64,128]{2,1,0:T(8,128)(2,1)} %bitcast.3), custom_call_target="tpu_custom_call" | custom-call | tf_op jit(solution)/shard_map/pallas_call | solution.py:440
  75.2 1.5 %shard_map.78 = (f32[16,8,64]{2,1,0:T(8,128)}, f32[16,8,64]{2,1,0:T(8,128)}) custom-call(f32[8,8,128]{2,1,0:T(8,128)} %get-tuple-element.4.pq, f32[8,8,128]{2,1,0:T(8,128)} %get-tuple-element.5.pk), custom_call_target="tpu_custom_call" | custom-call | tf_op jit(solution)/shard_map/pallas_call | solution.py:475
